TPU v7x, 32 devices: a whole 2x2x4 slice. The times are simulated.
32 devices in a mesh: lat: 8 (over y, x, core), lon: 4 (over z).
Axes of the slice: x: 2, y: 2, z: 4, core: 2. Of those that a mesh axis runs over, the one named last changes fastest.
Arguments:
- coeffs_old: float32 [640, 2, 3, 50, 640], P(('lat', 'lon')), may hold values from -0.16 to 0.16
- noise: bfloat16 [640, 2, 3, 50, 640], P(('lat', 'lon')), may hold values from -6 to 6
- legendre: float32 [640, 640, 640], P(('lat', 'lon')), may hold values from -0.25 to 0.25
- decay: float32 [3], replicated, may hold values from 0.3 to 0.97
- amplitude: float32 [3, 640], replicated, may hold values from 0.005 to 0.05
- wavenumber_of_slot: int32 [640], replicated, may hold values from 0 to 639, as said below
- lat_order: int32 [640], replicated, may hold values from 0 to 639, each once
Outputs:
- coeffs_new: float32 [640, 2, 3, 50, 640], P(('lat', 'lon'))
- pattern: float32 [640, 50, 1280], P(('lat', 'lon'))
Inputs may be any that keep to these rules, and one draw needn't show every extreme that they name: `wavenumber_of_slot`: every wavenumber fills exactly one slot; the sums of the wavenumbers of one device's 20 slots differ between devices by less than 32. `lat_order`: every latitude stands in exactly one row.
All inputs are finite; a program needn't handle non-finite values.
Results may differ from a plain program's by a relative error of at most 0.0003.
Values sent between devices are 32-bit elements; how exact they have to be, the bound alone decides.
A program may use at most 192 MiB of HBM per device.

v0:
```python
import jax
import jax.numpy as jnp
from jax import lax
from jax.sharding import PartitionSpec as P

LON = 1280
TWO_PI = 6.283185307179586


def evolve(coeffs_old, noise, decay, amplitude, waves):
    width = coeffs_old.shape[4]
    offsets = lax.broadcasted_iota(jnp.int32, (waves.shape[0], width), 1)
    live = waves[:, None] + offsets < width
    padded = jnp.concatenate([amplitude, jnp.zeros_like(amplitude)], axis=1)
    spread = jax.vmap(lambda wave: lax.dynamic_slice_in_dim(padded, wave, width, 1))(waves)
    factor = jnp.sqrt(1.0 - decay * decay)
    fresh = decay[None, None, :, None, None] * coeffs_old + (spread * factor[None, :, None])[
        :, None, :, None, :
    ] * noise.astype(jnp.float32)
    return jnp.where(live[:, None, None, None, :], fresh, jnp.zeros_like(fresh))


def synthesis_table(waves, length):
    column = lax.broadcasted_iota(jnp.int32, (waves.shape[0], length), 1)
    phase = waves[:, None] * column % length
    angle = phase.astype(jnp.float32) * (TWO_PI / length)
    weight = jnp.where(waves == 0, 1.0, 2.0).astype(jnp.float32)[:, None]
    return jnp.stack([weight * jnp.cos(angle), -weight * jnp.sin(angle)], axis=1)


def synthesize(values, table):
    return jnp.einsum("sreq,srl->qel", values, table, precision=lax.Precision.HIGHEST)


def local(coeffs_old, noise, legendre, decay, amplitude, wavenumber_of_slot, lat_order):
    lat_count = lax.axis_size("lat")
    lon_count = lax.axis_size("lon")
    lat_index = lax.axis_index("lat")
    lon_index = lax.axis_index("lon")
    slots = coeffs_old.shape[0]
    mine = lax.dynamic_slice_in_dim(
        wavenumber_of_slot, (lat_index * lon_count + lon_index) * slots, slots
    )
    coeffs_new = evolve(coeffs_old, noise, decay, amplitude, mine)
    field = jnp.einsum("srkej,slj->srel", coeffs_new, legendre, precision=lax.Precision.HIGHEST)
    field = jnp.take(field, lat_order, axis=3)
    ordered = wavenumber_of_slot.reshape(lat_count, lon_count, slots).transpose(1, 0, 2).reshape(-1)
    full_table = synthesis_table(ordered, LON)
    pattern = synthesize(
        lax.all_to_all(
            lax.all_to_all(field, "lat", split_axis=3, concat_axis=0, tiled=True),
            "lon",
            split_axis=3,
            concat_axis=0,
            tiled=True,
        ),
        full_table,
    )
    return (coeffs_new, pattern)


def solution(mesh):
    in_specs = (
        P(("lat", "lon"), None, None, None, None),
        P(("lat", "lon"), None, None, None, None),
        P(("lat", "lon"), None, None),
        P(),
        P(),
        P(),
        P(),
    )
    out_specs = (P(("lat", "lon"), None, None, None, None), P(("lat", "lon"), None, None))
    return jax.shard_map(local, mesh=mesh, in_specs=in_specs, out_specs=out_specs, check_vma=False)
```

profile of v0, /device:TPU:0, one launch (start us, length us, event | category | flops | bytes accessed | tf_op | source)
XLA Modules:
  0.0 590.6 jit_solution(11389839738425668350)
XLA Ops:
  2.0 0.8 fusion.12
  3.5 26.4 %while.1 = (s32[]{:T(128)}, f32[3,1280]{1,0:T(4,128)S(1)}, s32[20,2]{0,1:T(2,128)S(1)}, f32[20,3,640]{2,1,0:T(4,128)S(1)}, s32[]{:T(128)}) while((s32[]{:T(128)}, f32[3,1280]{1,0:T(4,128)S(1)}, s32[20,2]{0,1:T(2,128)S(1)}, f32[20,3,640]{2,1,0:T(4,128)S(1)}, s32[]{:T(128)}) %tuple.24), condition=%wide.while_cond, body=%wide.while_body.sunk | while | flops 2 | bytes 20585 | solution.py:15
  4.1 0.7 bitcast_dynamic-update-slice_fusion.2
  5.4 0.7 bitcast_dynamic-update-slice_fusion.2
  6.7 0.7 bitcast_dynamic-update-slice_fusion.2
  8.1 0.7 bitcast_dynamic-update-slice_fusion.2
  30.8 32.2 %fusion.15 = (f32[20,2,50,640]{3,1,2,0:T(2,128)}, f32[20,2,3,50,640]{4,1,3,2,0:T(2,128)}) fusion(bf16[20,2,3,50,640]{4,1,3,2,0:T(2,128)(2,1)} %param.8, f32[20,3,640]{2,1,0:T(4,128)S(1)} %broadcast_multiply_fusion, f32[20,2,3,50,640]{4,1,3,2,0:T(2,128)} %param.7, f32[3]{0:T(128)} %param.10, pred[20,640]{1,0:T(8,128)(4,1)S(1)} %add_compare_fusion), kind=kLoop, calls=%fused_computation.33 | loop fusion | flops 21760000 | bytes 43686412 | tf_op jit(solution)/shard_map/srkej,slj->srel/reduce_sum | solution.py:45
  63.0 36.1 %fusion = f32[20,2,50,640]{3,2,1,0:T(8,128)} fusion(f32[20,640,640]{2,1,0:T(8,128)} %param.9, f32[20,2,50,640]{3,1,2,0:T(2,128)} %get-tuple-element.18), kind=kOutput, calls=%fused_computation.3 | convolution fusion | flops 9830400000 | bytes 43008000 | tf_op jit(solution)/shard_map/srkej,slj->srel/dot_general | solution.py:45
  99.1 15.9 %copy.33 = f32[20,2,50,640]{2,1,3,0:T(2,128)} copy(f32[20,2,50,640]{3,2,1,0:T(8,128)} %fusion) | data formatting | bytes 10240000 | tf_op jit(solution)/shard_map/srkej,slj->srel/dot_general | solution.py:45
  115.0 38.6 %gather_fusion = f32[640,20,2,50]{3,2,1,0:T(2,128)} fusion(f32[20,2,50,640]{2,1,3,0:T(2,128)} %copy.33, s32[1024]{0:T(1024)S(1)} %pad_clamp_fusion), kind=kCustom, calls=%fused_computation | custom fusion | bytes 10242560 | tf_op jit(solution)/shard_map/jit(_take)/gather | solution.py:46
  153.6 10.2 %fusion.16 = f32[640,20,2,50]{3,2,1,0:T(2,128)} fusion(f32[640,20,2,50]{3,2,1,0:T(2,128)} %gather_fusion, pred[640]{0:T(1024)(128)(4,1)S(1)} %compare_and_fusion), kind=kLoop, calls=%fused_computation.34 | loop fusion | flops 1280000 | bytes 10240640
  163.8 27.8 %reshape.218 = f32[8,1,160000]{2,1,0:T(1,128)} reshape(f32[640,20,2,50]{3,2,1,0:T(2,128)} %fusion.16) | data formatting | bytes 10240000
  191.5 64.3 %all_to_all.36 = f32[8,1,160000]{2,1,0:T(1,128)} all-to-all(f32[8,1,160000]{2,1,0:T(1,128)} %reshape.218), channel_id=1, replica_groups=mesh['lat'=8,'lon'=4] {'lat'}, dimensions={0} | all-to-all | bytes 10240000 | tf_op jit(solution)/shard_map/all_to_all | solution.py:51
  256.3 17.0 %reduce = f32[8,160000]{1,0:T(8,128)} reduce(f32[8,1,160000]{2,1,0:T(1,128)} %all_to_all.36, f32[]{:T(128)} %broadcast.203), dimensions={1}, to_apply=%all_to_all.26.reduce_sub_computation | reduce | bytes 10240004 | tf_op jit(solution)/shard_map/all_to_all | solution.py:51
  273.3 33.3 %reshape.219 = f32[640,20,2,50]{3,2,1,0:T(2,128)} reshape(f32[8,160000]{1,0:T(8,128)} %reduce) | data formatting | bytes 10240000
  306.6 17.1 %copy.42 = f32[20,2,50,8,80]{4,3,1,2,0:T(8,128)} copy(f32[20,2,50,8,80]{2,1,0,4,3:T(2,128)} %bitcast.41) | data formatting | bytes 10240000 | tf_op jit(solution)/shard_map/all_to_all | solution.py:51
  323.7 13.0 %copy.35 = f32[8,20,2,50,80]{4,2,3,1,0:T(2,128)} copy(f32[8,20,2,50,80]{4,0,2,3,1:T(8,128)} %bitcast.43) | data formatting | bytes 10240000 | tf_op jit(solution)/shard_map/all_to_all | solution.py:51
  336.7 18.0 %copy.36 = f32[160,2,50,80]{0,1,2,3:T(2,128)} copy(f32[160,2,50,80]{3,1,2,0:T(2,128)} %bitcast.42) | data formatting | bytes 10240000 | tf_op jit(solution)/shard_map/all_to_all | solution.py:51
  354.7 5.7 all-to-all-start.1
  360.7 15.2 %cosine_multiply_fusion = (f32[640,1,1280]{2,0,1:T(8,128)S(1)}, f32[640,1,1280]{2,0,1:T(8,128)}) fusion(s32[640]{0:T(1024)S(1)} %reshape.185, f32[640]{0:T(1024)S(1)} %get-tuple-element.24, f32[640]{0:T(1024)S(1)} %get-tuple-element.25), kind=kLoop, calls=%fused_computation.17 | loop fusion | flops 9011200 | bytes 6561280 | tf_op jit(solution)/shard_map/mul | solution.py:28
  375.9 164.0 %all-to-all-done.1 = f32[160,2,50,80]{0,1,2,3:T(2,128)} async-done(((f32[160,2,50,80]{0,1,2,3:T(2,128)}), f32[160,2,50,80]{0,1,2,3:T(2,128)}, u32[]{:S(2)}, u32[]{:S(2)}) %all-to-all-start.1) | async-done | bytes 5120032 | tf_op jit(solution)/shard_map/all_to_all | solution.py:50
  539.9 11.8 %copy.44 = f32[4,160,2,50,20]{1,0,3,2,4:T(4,128)} copy(f32[4,160,2,50,20]{1,2,3,4,0:T(2,128)} %bitcast.11) | data formatting | bytes 10240000 | tf_op jit(solution)/shard_map/all_to_all | solution.py:50
  551.7 9.5 %reshape.217 = f32[640,2,50,20]{0,2,1,3:T(8,128)} reshape(f32[4,160,2,50,20]{1,0,3,2,4:T(4,128)} %copy.44) | data formatting | bytes 10240000 | tf_op jit(solution)/shard_map/all_to_all | solution.py:50
  561.3 29.1 %fusion.6 = f32[20,50,1280]{2,1,0:T(8,128)} fusion(f32[640,2,50,20]{0,2,1,3:T(8,128)} %reshape.217, f32[640,1,1280]{2,0,1:T(8,128)} %get-tuple-element.23, f32[640,1,1280]{2,0,1:T(8,128)S(1)} %get-tuple-element.22), kind=kOutput, calls=%fused_computation.13 | convolution fusion | flops 19662438400 | bytes 16793600 | tf_op jit(solution)/shard_map/sreq,srl->qel/dot_general | solution.py:32
  (72 shorter events, 27.2 us)
Async XLA Ops:
  354.7 5.8 copy-start
  354.7 185.2 %all-to-all-start.1 = ((f32[160,2,50,80]{0,1,2,3:T(2,128)}), f32[160,2,50,80]{0,1,2,3:T(2,128)}, u32[]{:S(2)}, u32[]{:S(2)}) async-start(f32[160,2,50,80]{0,1,2,3:T(2,128)} %copy.36), calls=%async_computation.1 | async-start | bytes 16384000 | tf_op jit(solution)/shard_map/all_to_all | solution.py:50
where the time goes:
time: 601 us; the launch traced here: 591 us
  local copies, waits for them, and re-layouts  213 us (35%)
  waiting for transfers between devices  164 us (27%)
  other arithmetic  77.6 us (13%)
  matrix products  65.2 us (11%)
  blocking collectives  64.3 us (11%)
    all_to_all x1, waiting for transfers between devices, local(): lax.all_to_all(lax.all_to_all(field, 'lat', split_axis=3, concat_axis=0,...  164 us
    all_to_all x1, blocking collectives, local(): lax.all_to_all(field, 'lat', split_axis=3, concat_axis=0, tiled=True)  64.3 us
    unnamed x4, local copies, waits for them, and re-layouts  61.1 us
    all_to_all x4, local copies, waits for them, and re-layouts, local(): lax.all_to_all(field, 'lat', split_axis=3, concat_axis=0, tiled=True)  48.6 us
    gather x1, local copies, waits for them, and re-layouts, local(): field = jnp.take(field, lat_order, axis=3)  38.6 us
    dot_general x1, matrix products, local(): jnp.einsum('srkej,slj->srel', coeffs_new, legendre, precision=lax.Precisi...  36.1 us
    reduce_sum x1, other arithmetic, local(): jnp.einsum('srkej,slj->srel', coeffs_new, legendre, precision=lax.Precisi...  32.2 us
    dot_general x1, matrix products, synthesize(): jnp.einsum('sreq,srl->qel', values, table, precision=lax.Precision.HIGHEST)  29.1 us
  transfers between devices with their start and end apart: 1, of which 1 were waited for; matrix products, arithmetic and copies ran while one was open for 3% of the time, Pallas kernels for 0%

commit v1 on v0

--- a/solution.py
+++ b/solution.py
@@ -48,7 +48,12 @@
     full_table = synthesis_table(ordered, LON)
     pattern = synthesize(
         lax.all_to_all(
-            lax.all_to_all(field, "lat", split_axis=3, concat_axis=0, tiled=True),
+            jnp.concatenate(
+                lax.all_to_all(
+                    jnp.stack(jnp.split(field, lax.axis_size("lat"), axis=3)), "lat", 0, 0
+                ),
+                axis=0,
+            ),
             "lon",
             split_axis=3,
             concat_axis=0,

time: 601 us -> 551 us (0.917); the launches traced: 591 us -> 548 us
  local copies, waits for them, and re-layouts: 213 us -> 154 us
  blocking collectives: 64.3 us -> 98.3 us
  other arithmetic: 77.6 us -> 59.6 us
    unnamed x4 -> x9, local copies, waits for them, and re-layouts: 61.1 us -> 9.09 us
    all_to_all x6 -> x2, local copies, waits for them, and re-layouts: 69.9 us -> 21.3 us  [local(): lax.all_to_all(jnp.concatenate(lax.all_to_all(jnp.stack(jnp.split(field,...]
    all_to_all x1, blocking collectives: 64.3 us -> 98.3 us  [local(): lax.all_to_all(jnp.stack(jnp.split(field, lax.axis_size('lat'), axis=3)),...]
    another operation x0 -> x2, local copies, waits for them, and re-layouts: none -> 23.9 us  [local(): jnp.stack(jnp.split(field, lax.axis_size('lat'), axis=3))]
    reshape x0 -> x1, local copies, waits for them, and re-layouts: none -> 18 us  [local(): jnp.concatenate(lax.all_to_all(jnp.stack(jnp.split(field, lax.axis_size('...]
    all_to_all x1 -> x0, other arithmetic: 17 us -> none  [local(): lax.all_to_all(field, 'lat', split_axis=3, concat_axis=0, tiled=True)]
    unnamed x2 -> x1, other arithmetic: 10.2 us -> 0.01 us
    select_n x1 -> x2, other arithmetic: 0.69 us -> 9.85 us  [local(): field = jnp.take(field, lat_order, axis=3)]
where the time goes in v1:
time: 551 us; the launch traced here: 548 us
  waiting for transfers between devices  164 us (30%)
  local copies, waits for them, and re-layouts  154 us (28%)
  blocking collectives  98.3 us (18%)
  matrix products  65 us (12%)
  other arithmetic  59.6 us (11%)
  starting transfers between devices  5.96 us (1%)
    all_to_all x1, waiting for transfers between devices, local(): lax.all_to_all(jnp.concatenate(lax.all_to_all(jnp.stack(jnp.split(field,...  164 us
    all_to_all x1, blocking collectives, local(): lax.all_to_all(jnp.stack(jnp.split(field, lax.axis_size('lat'), axis=3)),...  98.3 us
    gather x1, local copies, waits for them, and re-layouts, local(): field = jnp.take(field, lat_order, axis=3)  38.6 us
    dot_general x1, matrix products, local(): jnp.einsum('srkej,slj->srel', coeffs_new, legendre, precision=lax.Precisi...  36.1 us
    reduce_sum x1, other arithmetic, local(): jnp.einsum('srkej,slj->srel', coeffs_new, legendre, precision=lax.Precisi...  32.2 us
    dot_general x1, matrix products, synthesize(): jnp.einsum('sreq,srl->qel', values, table, precision=lax.Precision.HIGHEST)  28.9 us
    gather x60, local copies, waits for them, and re-layouts  26.4 us
    another operation x2, local copies, waits for them, and re-layouts, local(): jnp.stack(jnp.split(field, lax.axis_size('lat'), axis=3))  23.9 us
  transfers between devices with their start and end apart: 1, of which 1 were waited for; matrix products, arithmetic and copies ran while one was open for 3% of the time, Pallas kernels for 0%

profile of v1, /device:TPU:0, one launch (start us, length us, event | category | flops | bytes accessed | tf_op | source)
XLA Modules:
  0.0 548.0 jit_solution(2393428800962391764)
XLA Ops:
  2.0 0.8 fusion.20
  3.5 26.4 %while.1 = (s32[]{:T(128)}, f32[3,1280]{1,0:T(4,128)S(1)}, s32[20,2]{0,1:T(2,128)S(1)}, f32[20,3,640]{2,1,0:T(4,128)S(1)}, s32[]{:T(128)}) while((s32[]{:T(128)}, f32[3,1280]{1,0:T(4,128)S(1)}, s32[20,2]{0,1:T(2,128)S(1)}, f32[20,3,640]{2,1,0:T(4,128)S(1)}, s32[]{:T(128)}) %tuple.24), condition=%wide.while_cond, body=%wide.while_body.sunk | while | flops 2 | bytes 20585 | solution.py:15
  30.8 32.2 %fusion.23 = (f32[20,2,50,640]{3,1,2,0:T(2,128)}, f32[20,2,3,50,640]{4,1,3,2,0:T(2,128)}) fusion(bf16[20,2,3,50,640]{4,1,3,2,0:T(2,128)(2,1)} %param.8, f32[20,3,640]{2,1,0:T(4,128)S(1)} %broadcast_multiply_fusion, f32[20,2,3,50,640]{4,1,3,2,0:T(2,128)} %param.7, f32[3]{0:T(128)} %param.10, pred[20,640]{1,0:T(8,128)(4,1)S(1)} %add_compare_fusion), kind=kLoop, calls=%fused_computation.49 | loop fusion | flops 21760000 | bytes 43686412 | tf_op jit(solution)/shard_map/srkej,slj->srel/reduce_sum | solution.py:45
  63.0 36.1 %fusion = f32[20,2,50,640]{3,2,1,0:T(8,128)} fusion(f32[20,640,640]{2,1,0:T(8,128)} %param.9, f32[20,2,50,640]{3,1,2,0:T(2,128)} %get-tuple-element.18), kind=kOutput, calls=%fused_computation.3 | convolution fusion | flops 9830400000 | bytes 43008000 | tf_op jit(solution)/shard_map/srkej,slj->srel/dot_general | solution.py:45
  99.1 15.9 %copy.29 = f32[20,2,50,640]{2,1,3,0:T(2,128)} copy(f32[20,2,50,640]{3,2,1,0:T(8,128)} %fusion) | data formatting | bytes 10240000 | tf_op jit(solution)/shard_map/srkej,slj->srel/dot_general | solution.py:45
  115.0 38.6 %gather_fusion = f32[640,20,2,50]{3,2,1,0:T(2,128)} fusion(f32[20,2,50,640]{2,1,3,0:T(2,128)} %copy.29, s32[1024]{0:T(1024)S(1)} %pad_clamp_fusion), kind=kCustom, calls=%fused_computation | custom fusion | bytes 10242560 | tf_op jit(solution)/shard_map/jit(_take)/gather | solution.py:46
  153.6 9.2 %select_bitcast_fusion = f32[20,2,50,640]{2,1,0,3:T(2,128)S(1)} fusion(f32[640,20,2,50]{3,2,1,0:T(2,128)} %gather_fusion, pred[640]{0:T(1024)(128)(4,1)S(1)} %compare_and_fusion), kind=kLoop, calls=%fused_computation.6 | loop fusion | flops 1280000 | bytes 10240640 | tf_op jit(solution)/shard_map/jit(_take)/select_n | solution.py:46
  162.7 1.3 fusion.19
  164.0 1.3 fusion.18
  165.3 1.3 fusion.17
  166.6 1.3 fusion.16
  167.9 1.3 fusion.15
  169.2 1.4 fusion.14
  170.6 1.3 fusion.13
  171.8 1.3 fusion.12
  173.2 22.6 %copy.30 = f32[8,20,2,50,80]{4,2,3,1,0:T(2,128)} copy(f32[8,20,2,50,80]{3,2,1,4,0:T(2,128)} %fusion.12) | data formatting | bytes 10240000 | tf_op jit(solution)/shard_map/stack | solution.py:53
  195.8 98.3 %all_to_all.23 = f32[8,20,2,50,80]{4,2,3,1,0:T(2,128)} all-to-all(f32[8,20,2,50,80]{4,2,3,1,0:T(2,128)} %copy.30), channel_id=1, replica_groups=mesh['lat'=8,'lon'=4] {'lat'}, dimensions={0} | all-to-all | bytes 10240000 | tf_op jit(solution)/shard_map/all_to_all | solution.py:52
  294.0 18.0 %copy.31 = f32[160,2,50,80]{0,1,2,3:T(2,128)} copy(f32[160,2,50,80]{3,1,2,0:T(2,128)} %bitcast.66) | data formatting | bytes 10240000 | tf_op jit(solution)/shard_map/reshape | solution.py:51
  312.0 6.0 %all-to-all-start.1 = ((f32[160,2,50,80]{0,1,2,3:T(2,128)}), f32[160,2,50,80]{0,1,2,3:T(2,128)}, u32[]{:S(2)}, u32[]{:S(2)}) async-start(f32[160,2,50,80]{0,1,2,3:T(2,128)} %copy.31), calls=%async_computation.1 | async-start | bytes 16384000 | tf_op jit(solution)/shard_map/all_to_all | solution.py:50
  318.2 15.2 %cosine_multiply_fusion = (f32[640,1,1280]{2,0,1:T(8,128)S(1)}, f32[640,1,1280]{2,0,1:T(8,128)}) fusion(s32[640]{0:T(1024)S(1)} %reshape.188, f32[640]{0:T(1024)S(1)} %get-tuple-element.24, f32[640]{0:T(1024)S(1)} %get-tuple-element.25), kind=kLoop, calls=%fused_computation.17 | loop fusion | flops 9011200 | bytes 6561280 | tf_op jit(solution)/shard_map/mul | solution.py:28
  333.4 164.3 %all-to-all-done.1 = f32[160,2,50,80]{0,1,2,3:T(2,128)} async-done(((f32[160,2,50,80]{0,1,2,3:T(2,128)}), f32[160,2,50,80]{0,1,2,3:T(2,128)}, u32[]{:S(2)}, u32[]{:S(2)}) %all-to-all-start.1) | async-done | bytes 5120032 | tf_op jit(solution)/shard_map/all_to_all | solution.py:50
  497.7 11.8 %copy.38 = f32[4,160,2,50,20]{1,0,3,2,4:T(4,128)} copy(f32[4,160,2,50,20]{1,2,3,4,0:T(2,128)} %bitcast.17) | data formatting | bytes 10240000 | tf_op jit(solution)/shard_map/all_to_all | solution.py:50
  509.5 9.6 %reshape.221 = f32[640,2,50,20]{0,2,1,3:T(8,128)} reshape(f32[4,160,2,50,20]{1,0,3,2,4:T(4,128)} %copy.38) | data formatting | bytes 10240000 | tf_op jit(solution)/shard_map/all_to_all | solution.py:50
  519.1 28.9 %fusion.6 = f32[20,50,1280]{2,1,0:T(8,128)} fusion(f32[640,2,50,20]{0,2,1,3:T(8,128)} %reshape.221, f32[640,1,1280]{2,0,1:T(8,128)} %get-tuple-element.23, f32[640,1,1280]{2,0,1:T(8,128)S(1)} %get-tuple-element.22), kind=kOutput, calls=%fused_computation.13 | convolution fusion | flops 19662438400 | bytes 16793600 | tf_op jit(solution)/shard_map/sreq,srl->qel/dot_general | solution.py:32
  (75 shorter events, 29.5 us)
Async XLA Ops:
  312.0 6.0 %copy-start = (s32[640]{0:T(1024)S(1)}, s32[640]{0:T(1024)}, u32[]{:S(2)}) copy-start(s32[640]{0:T(1024)} %param.12) | copy-start | bytes 7684
  312.0 185.7 %all-to-all-start.1 = ((f32[160,2,50,80]{0,1,2,3:T(2,128)}), f32[160,2,50,80]{0,1,2,3:T(2,128)}, u32[]{:S(2)}, u32[]{:S(2)}) async-start(f32[160,2,50,80]{0,1,2,3:T(2,128)} %copy.31), calls=%async_computation.1 | async-start | bytes 16384000 | tf_op jit(solution)/shard_map/all_to_all | solution.py:50
